TPU v7x, 32 devices: a whole 2x2x4 slice. The times are simulated.
32 devices in a mesh: blk: 32 (over z, y, x, core).
Axes of the slice: x: 2, y: 2, z: 4, core: 2. Of those that a mesh axis runs over, the one named last changes fastest.
Arguments:
- frames: float32 [128, 128, 1280], P('blk'), may hold values from -6 to 6
- widths: float32 [128], replicated, may hold values from 2 to 12
- kernel: float32 [3, 3], replicated, may hold values from -3 to 3
Outputs:
- filtered: float32 [128, 128, 1280], P(None, 'blk')
All inputs are finite; a program needn't handle non-finite values.
Results may differ from a plain program's by a relative error of at most 0.00007.
Values sent between devices are 32-bit elements; how exact they have to be, the bound alone decides.
A program may use at most 64 MiB of HBM per device.

v0:
```python
import functools

import jax
import jax.numpy as jnp
from jax import lax
from jax.experimental import pallas as pl
from jax.experimental.pallas import tpu as pltpu
from jax.sharding import PartitionSpec as P

BAND = 24
MESH = pl.DeviceIdType.MESH


def exchange_kernel(
    n,
    frames_ref,
    widths_hbm,
    kernel_hbm,
    out_ref,
    held,
    window,
    outgoing,
    incoming,
    mixing,
    widths_ref,
    kernel_ref,
    in_sem,
    send_sem,
    recv_sem,
    relay_sem,
):
    per_device, height, columns = frames_ref.shape
    chunks, _, rows_block, chunk = outgoing.shape
    rows = rows_block // per_device
    group = 8 // rows
    groups = n // group
    length = widths_ref.shape[1]
    me = lax.axis_index("blk")
    quarter = n // 4
    mine = me // quarter
    place = me - mine * quarter
    mirror = 3 - mine
    beside = mine + 1 - 2 * lax.rem(mine, 2)
    across = mirror + 1 - 2 * lax.rem(mirror, 2)
    partner = beside * quarter + place
    opposite = mirror * quarter + place

    strip = height // 4
    first = mirror * strip
    above = jnp.where(mirror == 0, 0, first - 8)
    below = jnp.where(mirror == 3, height - 8, first + strip)

    def load(source, rows_in, target, at, semaphore):
        return pltpu.make_async_copy(
            frames_ref.at[:, pl.ds(pl.multiple_of(source, 8), rows_in), :],
            target.at[:, pl.ds(at, rows_in), :],
            semaphore,
        )

    early = [
        pltpu.make_async_copy(kernel_hbm, kernel_ref, in_sem.at[1]),
        load(first, strip, window, 8, in_sem.at[3]),
        load(above, 8, window, 0, in_sem.at[4]),
        load(below, 8, window, strip + 8, in_sem.at[5]),
    ]
    late = [
        load(0, height, held, 8, in_sem.at[0]),
        pltpu.make_async_copy(widths_hbm, widths_ref, in_sem.at[2]),
    ]
    for copy in early:
        copy.start()

    def signal(semaphore, target):
        pl.semaphore_signal(
            semaphore, inc=1, device_id=(target,), device_id_type=MESH
        )

    barrier = pltpu.get_barrier_semaphore()

    @pl.loop(0, quarter)
    def _(step):
        signal(barrier, mirror * quarter + lax.rem(place + step, quarter))

    signal(barrier, partner)

    edge = jnp.zeros((per_device, 8, columns), jnp.float32)
    held[:, pl.ds(0, 8), :] = edge
    held[:, pl.ds(height + 8, 8), :] = edge
    for copy in early:
        copy.wait()
    for copy in late:
        copy.start()

    @pl.when(mirror == 0)
    def _():
        window[:, pl.ds(0, 8), :] = edge

    @pl.when(mirror == 3)
    def _():
        window[:, pl.ds(strip + 8, 8), :] = edge

    part = quarter // group
    own = me // group
    seat = place // group

    def group_at(which, step):
        return which * part + lax.rem(seat + step, part)

    column = lax.broadcasted_iota(jnp.int32, (8, columns), 1)

    def filter_group(at, source, base):
        for frame in range(per_device):
            tall = source[frame, pl.ds(pl.multiple_of((at - base) * 8, 8), 24), :]
            taps = [tall[7:15], tall[8:16], tall[9:17]]
            mixed = [
                kernel_ref[0, col] * taps[0]
                + kernel_ref[1, col] * taps[1]
                + kernel_ref[2, col] * taps[2]
                for col in range(3)
            ]
            left = jnp.where(column == 0, 0.0, pltpu.roll(mixed[0], 1, 1))
            right = jnp.where(
                column == columns - 1, 0.0, pltpu.roll(mixed[2], columns - 1, 1)
            )
            value = left + mixed[1] + right
            for member in range(group):
                for k in range(chunks):
                    outgoing[
                        k, at * group + member, pl.ds(frame * rows, rows), :
                    ] = value[
                        member * rows : (member + 1) * rows,
                        k * chunk : (k + 1) * chunk,
                    ]

    def send(k, target):
        pltpu.make_async_remote_copy(
            src_ref=outgoing.at[k, target],
            dst_ref=incoming.at[k, me],
            send_sem=send_sem.at[k],
            recv_sem=recv_sem.at[k],
            device_id=(target,),
            device_id_type=MESH,
        ).start()

    def send_own_group(k):
        for other in range(1, group):
            send(k, own * group + lax.rem(me + other, group))
        pltpu.make_async_copy(
            outgoing.at[k, me], incoming.at[k, me], recv_sem.at[k]
        ).start()

    def filter_quarter(which):
        @pl.loop(0, part)
        def _(step):
            filter_group(group_at(which, step), held, 0)

    def send_quarter(which, k):
        @pl.loop(0, part)
        def _(step):
            at = group_at(which, step)
            for member in range(group):
                send(k, at * group + member)

    def send_near(k):
        @pl.loop(1, part)
        def _(step):
            at = group_at(mine, step)
            for member in range(group):
                send(k, at * group + member)

        send_own_group(k)

    def filter_early(step):
        filter_group(group_at(mirror, step), window, mirror * part)

    def send_early(step):
        at = group_at(mirror, step)

        @pl.loop(0, opening)
        def _(k):
            for member in range(group):
                send(k, at * group + member)

    opening = min(2, chunks)
    inner = (mine == 1) | (mine == 2)
    filter_early(0)
    pl.semaphore_wait(barrier, quarter + 1)
    signal(relay_sem.at[0], partner)

    @pl.loop(0, part - 1)
    def _(step):
        send_early(step)
        filter_early(step + 1)

    send_early(part - 1)
    for copy in late:
        copy.wait()
    filter_quarter(across)
    pl.semaphore_wait(relay_sem.at[0], 1)
    signal(relay_sem.at[1], opposite)

    def send_mirror():
        @pl.loop(opening, chunks)
        def _(k):
            send_quarter(mirror, k)

    def send_across():
        @pl.loop(0, chunks)
        def _(k):
            send_quarter(across, k)

    pl.when(inner)(send_across)
    pl.when(jnp.logical_not(inner))(send_mirror)
    filter_quarter(beside)
    filter_quarter(mine)
    pl.semaphore_wait(relay_sem.at[1], 1)

    @pl.loop(0, chunks)
    def _(k):
        send_quarter(beside, k)
        send_near(k)

    pl.when(inner)(send_mirror)
    pl.when(jnp.logical_not(inner))(send_across)

    total = length * rows
    target_at = lax.broadcasted_iota(jnp.int32, (total, length), 0) // rows
    lane = lax.broadcasted_iota(jnp.int32, (total, length), 1)
    spread = jnp.sum(
        jnp.where(target_at == lane, widths_ref[...], 0.0), axis=1, keepdims=True
    )
    row_at = lax.broadcasted_iota(jnp.int32, (total, total), 0)
    col_at = lax.broadcasted_iota(jnp.int32, (total, total), 1)
    apart = row_at // rows - col_at // rows
    inside = (jnp.abs(apart) <= BAND) & (row_at % rows == col_at % rows)
    offset = apart.astype(jnp.float32)
    weights = jnp.where(
        inside, jnp.exp(-offset * offset / (2.0 * spread * spread)), 0.0
    )
    mixing[...] = weights / jnp.sum(weights, axis=1, keepdims=True)

    @pl.loop(0, chunks)
    def _(k):
        pltpu.make_async_copy(incoming.at[k], incoming.at[k], recv_sem.at[k]).wait()
        if rows_block % 8 == 0:
            block = incoming[k].reshape(total, chunk)
        else:
            block = jnp.concatenate([incoming[k, s] for s in range(n)], axis=0)
        out_ref[:, pl.ds(pl.multiple_of(k * chunk, 128), chunk)] = jnp.dot(
            mixing[...],
            block,
            precision=lax.Precision.HIGHEST,
            preferred_element_type=jnp.float32,
        )

    @pl.loop(0, chunks)
    def _(k):
        sent = outgoing.at[k, pl.ds(0, n - 1)]
        pltpu.make_async_copy(sent, sent, send_sem.at[k]).wait()


def local(n, frames, widths, kernel):
    per_device, height, columns = frames.shape
    length = widths.shape[0]
    rows = height // n
    chunk = 256 if columns % 256 == 0 else 128
    chunks = columns // chunk
    vmem = pl.BlockSpec(memory_space=pltpu.VMEM)
    mixed = pl.pallas_call(
        functools.partial(exchange_kernel, n),
        out_shape=jax.ShapeDtypeStruct((length * rows, columns), jnp.float32),
        in_specs=[pl.BlockSpec(memory_space=pltpu.HBM)] * 3,
        out_specs=vmem,
        scratch_shapes=[
            pltpu.VMEM((per_device, height + 16, columns), jnp.float32),
            pltpu.VMEM((per_device, height // 4 + 16, columns), jnp.float32),
            pltpu.VMEM((chunks, n, per_device * rows, chunk), jnp.float32),
            pltpu.VMEM((chunks, n, per_device * rows, chunk), jnp.float32),
            pltpu.VMEM((length * rows, length * rows), jnp.float32),
            pltpu.VMEM((1, length), jnp.float32),
            pltpu.SMEM((3, 3), jnp.float32),
            pltpu.SemaphoreType.DMA((6,)),
            pltpu.SemaphoreType.DMA((chunks,)),
            pltpu.SemaphoreType.DMA((chunks,)),
            pltpu.SemaphoreType.REGULAR((2,)),
        ],
        compiler_params=pltpu.CompilerParams(
            collective_id=0,
            has_side_effects=True,
            vmem_limit_bytes=50 * 1024 * 1024,
        ),
    )(frames, widths.reshape(1, length), kernel)
    return mixed.reshape(length, rows, columns)


def solution(mesh):
    return jax.shard_map(
        functools.partial(local, mesh.shape["blk"]),
        mesh=mesh,
        in_specs=(P("blk", None, None), P(), P()),
        out_specs=P(None, "blk", None),
        check_vma=False,
    )
```

profile of v0, /device:TPU:9, one launch (start us, length us, event | category | flops | bytes accessed | tf_op | source)
XLA Modules:
  0.0 65.7 jit_solution(13935964290258009035)
XLA Ops:
  0.0 0.0 copy-start
  0.0 0.7 %copy-done = f32[3,3]{1,0:T(4,128)S(1)} copy-done((f32[3,3]{1,0:T(4,128)S(1)}, f32[3,3]{1,0:T(4,128)}, u32[]{:S(2)}) %copy-start) | copy-done | bytes 60
  0.7 0.0 copy-start.1
  0.7 0.7 copy-done.1
  1.3 62.5 %shard_map.37 = f32[512,1280]{1,0:T(8,128)S(1)} custom-call(f32[4,128,1280]{2,1,0:T(8,128)} %frames_ref.1, f32[1,128]{1,0:T(1,128)S(1)} %bitcast.1, f32[3,3]{1,0:T(4,128)S(1)} %copy-done), custom_call_target="tpu_custom_call" | custom-call | tf_op jit(solution)/shard_map/pallas_call | solution.py:269
  63.8 1.9 %reshape.7 = f32[128,4,1280]{2,1,0:T(4,128)} reshape(f32[512,1280]{1,0:T(8,128)S(1)} %shard_map.37) | data formatting | bytes 5242880 | tf_op jit(solution)/shard_map/reshape | solution.py:293
Async XLA Ops:
  0.0 0.7 %copy-start = (f32[3,3]{1,0:T(4,128)S(1)}, f32[3,3]{1,0:T(4,128)}, u32[]{:S(2)}) copy-start(f32[3,3]{1,0:T(4,128)} %kernel_hbm.1) | copy-start | bytes 112
  0.7 0.7 copy-start.1
where the time goes:
time: 65.9 us; the launch traced here: 65.7 us
  Pallas kernels  62.5 us (95%)
  local copies, waits for them, and re-layouts  3.23 us (5%)
    pallas_call x1, Pallas kernels, local(): pl.pallas_call(functools.partial(exchange_kernel, n), out_shape=jax.Shape...  62.5 us
    reshape x1, local copies, waits for them, and re-layouts, local(): return mixed.reshape(length, rows, columns)  1.89 us
    unnamed x4, local copies, waits for them, and re-layouts  1.34 us

commit v1 on v0

--- a/solution.py
+++ b/solution.py
@@ -246,17 +246,30 @@
             block = incoming[k].reshape(total, chunk)
         else:
             block = jnp.concatenate([incoming[k, s] for s in range(n)], axis=0)
-        out_ref[:, pl.ds(pl.multiple_of(k * chunk, 128), chunk)] = jnp.dot(
+        mixed = jnp.dot(
             mixing[...],
             block,
             precision=lax.Precision.HIGHEST,
             preferred_element_type=jnp.float32,
         )
+        out_ref[:, :, pl.ds(pl.multiple_of(k * chunk, 128), chunk)] = mixed.reshape(
+            length, rows, chunk
+        )
 
     @pl.loop(0, chunks)
     def _(k):
         sent = outgoing.at[k, pl.ds(0, n - 1)]
         pltpu.make_async_copy(sent, sent, send_sem.at[k]).wait()
+
+
+def write_kernel(mixed_ref, out_ref, sem):
+    copy = pltpu.make_async_copy(mixed_ref, out_ref, sem)
+    copy.start()
+    copy.wait()
+
+
+def in_hbm(array):
+    return pltpu.with_memory_space_constraint(array, pltpu.HBM)
 
 
 def local(n, frames, widths, kernel):
@@ -265,11 +278,13 @@
     rows = height // n
     chunk = 256 if columns % 256 == 0 else 128
     chunks = columns // chunk
+    hbm = pl.BlockSpec(memory_space=pltpu.HBM)
     vmem = pl.BlockSpec(memory_space=pltpu.VMEM)
+    shape = (length, rows, columns)
     mixed = pl.pallas_call(
         functools.partial(exchange_kernel, n),
-        out_shape=jax.ShapeDtypeStruct((length * rows, columns), jnp.float32),
-        in_specs=[pl.BlockSpec(memory_space=pltpu.HBM)] * 3,
+        out_shape=pltpu.VMEM(shape, jnp.float32),
+        in_specs=[hbm] * 3,
         out_specs=vmem,
         scratch_shapes=[
             pltpu.VMEM((per_device, height + 16, columns), jnp.float32),
@@ -289,8 +304,15 @@
             has_side_effects=True,
             vmem_limit_bytes=50 * 1024 * 1024,
         ),
-    )(frames, widths.reshape(1, length), kernel)
-    return mixed.reshape(length, rows, columns)
+    )(in_hbm(frames), in_hbm(widths.reshape(1, length)), in_hbm(kernel))
+    return pl.pallas_call(
+        write_kernel,
+        out_shape=pltpu.HBM(shape, jnp.float32),
+        in_specs=[vmem],
+        out_specs=hbm,
+        scratch_shapes=[pltpu.SemaphoreType.DMA],
+        compiler_params=pltpu.CompilerParams(vmem_limit_bytes=1024 * 1024),
+    )(mixed)
 
 
 def solution(mesh):

time: 65.9 us -> 64.2 us (0.974)
  local copies, waits for them, and re-layouts: 3.23 us -> 0 us
  Pallas kernels: 62.5 us -> 64 us
    reshape x1 -> x0, local copies, waits for them, and re-layouts: 1.89 us -> none  [local(): return mixed.reshape(length, rows, columns)]
    pallas_call x1 -> x2, Pallas kernels: 62.5 us -> 64 us  [the longest x1 62.5 us: local(): pl.pallas_call(functools.partial(exchange_kernel, n), out_shape=pltpu.VME...]
    unnamed x4 -> x0, local copies, waits for them, and re-layouts: 1.34 us -> none
where the time goes in v1:
time: 64.2 us; the launch traced here: 64 us
  Pallas kernels  64 us (100%)
    pallas_call x1, Pallas kernels, local(): pl.pallas_call(functools.partial(exchange_kernel, n), out_shape=pltpu.VME...  62.5 us
    pallas_call x1, Pallas kernels, local(): pl.pallas_call(write_kernel, out_shape=pltpu.HBM(shape, jnp.float32), in_...  1.5 us

profile of v1, /device:TPU:9, one launch (start us, length us, event | category | flops | bytes accessed | tf_op | source)
XLA Modules:
  0.0 64.0 jit_solution(17356065158998995041)
XLA Ops:
  0.0 62.5 %shard_map.37.mixed_ref = f32[128,4,1280]{2,1,0:T(4,128)S(1)} custom-call(f32[4,128,1280]{2,1,0:T(8,128)} %frames_ref.1, f32[1,128]{1,0:T(1,128)} %bitcast.1, f32[3,3]{1,0:T(4,128)} %kernel_hbm.1), custom_call_target="tpu_custom_call" | custom-call | tf_op jit(solution)/shard_map/pallas_call | solution.py:284
  62.5 1.5 %shard_map.38 = f32[128,4,1280]{2,1,0:T(4,128)} custom-call(f32[128,4,1280]{2,1,0:T(4,128)S(1)} %shard_map.37.mixed_ref), custom_call_target="tpu_custom_call" | custom-call | tf_op jit(solution)/shard_map/pallas_call | solution.py:308

commit v2 on v1

v2 whole, which is shorter than its diff:
```python
import functools

import jax
import jax.numpy as jnp
from jax import lax
from jax.experimental import pallas as pl
from jax.experimental.pallas import tpu as pltpu
from jax.sharding import PartitionSpec as P

BAND = 24
LAYERS = 4
MESH = pl.DeviceIdType.MESH


def exchange_kernel(
    n,
    frames_ref,
    widths_hbm,
    kernel_hbm,
    out_ref,
    held,
    window,
    opening,
    outgoing,
    incoming,
    mixing,
    partial,
    widths_ref,
    kernel_ref,
    in_sem,
    send_sem,
    recv_sem,
    round_sem,
):
    per_device, height, columns = frames_ref.shape
    chunks, _, rows_block, chunk = outgoing.shape
    rows = rows_block // per_device
    group = 8 // rows
    length = widths_ref.shape[1]
    me = lax.axis_index("blk")
    quarter = n // LAYERS
    mine = me // quarter
    place = me - mine * quarter
    mirror = 3 - mine
    beside = mine + 1 - 2 * lax.rem(mine, 2)
    across = mirror + 1 - 2 * lax.rem(mirror, 2)
    inner = (mine == 1) | (mine == 2)
    outer = jnp.logical_not(inner)
    front = jnp.where(inner, mirror, beside)
    opposite = mirror * quarter + place
    partner = beside * quarter + place
    part = quarter // group
    seat = place // group
    member_of = place - seat * group
    bits = part.bit_length() - 1
    core_bits = group.bit_length() - 1
    steps = core_bits + bits
    arrived = round_sem.at[2 * steps]
    meet = round_sem.at[2 * steps + 1]
    relay = round_sem.at[2 * steps + 2]

    def flip(value, step):
        return value + step - 2 * step * lax.rem(value // step, 2)

    def mixed_seat(step):
        return lax.rem(seat + step, part)

    strip = height // LAYERS
    first = front * strip

    def load(source, rows_in, target, at, semaphore):
        return pltpu.make_async_copy(
            frames_ref.at[:, pl.ds(pl.multiple_of(source, 8), rows_in), :],
            target.at[:, pl.ds(at, rows_in), :],
            semaphore,
        )

    early = [
        pltpu.make_async_copy(kernel_hbm, kernel_ref, in_sem.at[0]),
        load(first + seat * 8 - 8, 24, opening, 0, in_sem.at[1]),
    ]
    front_load = load(first - 8, strip + 16, window, 0, in_sem.at[2])
    late = [
        load(0, height, held, 8, in_sem.at[3]),
        pltpu.make_async_copy(widths_hbm, widths_ref, in_sem.at[4]),
    ]
    for copy in early:
        copy.start()

    def signal(semaphore, target):
        pl.semaphore_signal(
            semaphore, inc=1, device_id=(target,), device_id_type=MESH
        )

    barrier = pltpu.get_barrier_semaphore()
    neighbours = [flip(place, 1 << bit) for bit in range(core_bits + bits)]
    for place_at in neighbours:
        signal(barrier, mine * quarter + place_at)

    @pl.when(inner)
    def _():
        for layer in (mirror, beside):
            for member in range(group):
                signal(barrier, layer * quarter + seat * group + member)

    edge = jnp.zeros((per_device, 8, columns), jnp.float32)
    held[:, pl.ds(0, 8), :] = edge
    held[:, pl.ds(height + 8, 8), :] = edge
    column = lax.broadcasted_iota(jnp.int32, (8, columns), 1)

    def filter_group(at, source, base):
        for frame in range(per_device):
            start = (at - base) * 8
            if not isinstance(start, int):
                start = pl.multiple_of(start, 8)
            tall = source[frame, pl.ds(start, 24), :]
            taps = [tall[7:15], tall[8:16], tall[9:17]]
            mixed = [
                kernel_ref[0, col] * taps[0]
                + kernel_ref[1, col] * taps[1]
                + kernel_ref[2, col] * taps[2]
                for col in range(3)
            ]
            left = jnp.where(column == 0, 0.0, pltpu.roll(mixed[0], 1, 1))
            right = jnp.where(
                column == columns - 1, 0.0, pltpu.roll(mixed[2], columns - 1, 1)
            )
            value = left + mixed[1] + right
            for member in range(group):
                for k in range(chunks):
                    outgoing[
                        k, at * group + member, pl.ds(frame * rows, rows), :
                    ] = value[
                        member * rows : (member + 1) * rows,
                        k * chunk : (k + 1) * chunk,
                    ]

    def send(k, target):
        pltpu.make_async_remote_copy(
            src_ref=outgoing.at[k, target],
            dst_ref=incoming.at[k, me],
            send_sem=send_sem.at[k],
            recv_sem=recv_sem.at[k, mine],
            device_id=(target,),
            device_id_type=MESH,
        ).start()

    def send_group(at):
        @pl.loop(0, chunks)
        def _(k):
            for member in range(group):
                send(k, at * group + member)

    def send_quarter_at(which, k):
        @pl.loop(0, part)
        def _(step):
            at = which * part + mixed_seat(step)
            for member in range(group):
                send(k, at * group + member)

    def send_quarter(which):
        @pl.loop(0, chunks)
        def _(k):
            send_quarter_at(which, k)

    def send_front_at(k):
        @pl.loop(1, part)
        def _(step):
            at = front * part + mixed_seat(step)
            for member in range(group):
                send(k, at * group + member)

    def send_front(begin, end):
        @pl.loop(begin, end)
        def _(k):
            send_front_at(k)

    def send_near_at(k):
        @pl.loop(1, part)
        def _(step):
            at = mine * part + mixed_seat(step)
            for member in range(group):
                send(k, at * group + member)

        for other in range(1, group):
            send(
                k,
                mine * quarter
                + seat * group
                + lax.rem(member_of + other, group),
            )
        pltpu.make_async_copy(
            outgoing.at[k, me], incoming.at[k, me], recv_sem.at[k, mine]
        ).start()

    def filter_quarter(which):
        @pl.loop(0, part)
        def _(step):
            filter_group(which * part + mixed_seat(step), held, 0)

    for copy in early:
        copy.wait()
    front_load.start()
    for copy in late:
        copy.start()
    own = front * part + seat
    filter_group(own, opening, own)
    pl.semaphore_wait(barrier, group + core_bits + bits)
    send_group(own)

    @pl.when(outer)
    def _():
        signal(arrived, partner)

    def pass_on(bit, at):
        signal(at, mine * quarter + neighbours[bit])

    for bit in range(core_bits):
        pass_on(bit, round_sem.at[bit])
        pl.semaphore_wait(round_sem.at[bit], 1)
    front_load.wait()
    for bit in range(bits):
        at = round_sem.at[core_bits + bit]
        pass_on(core_bits + bit, at)

        @pl.loop(1 << bit, 2 << bit)
        def _(step):
            filter_group(front * part + mixed_seat(step), window, front * part)

        pl.semaphore_wait(at, 1)

    split = jnp.where(inner, min(2, chunks), 0)
    send_front(0, split)
    for copy in late:
        copy.wait()

    @pl.when(inner)
    def _():
        pl.semaphore_wait(arrived, 1)
        for bit in range(steps):
            at = round_sem.at[steps + bit]
            pass_on(bit, at)
            if bit < part:
                filter_group(across * part + mixed_seat(bit), held, 0)
            pl.semaphore_wait(at, 1)
        signal(meet, opposite)

        @pl.loop(min(steps, part), part)
        def _(step):
            filter_group(across * part + mixed_seat(step), held, 0)

        pl.semaphore_wait(meet, 1)
        signal(relay, partner)
        send_quarter(across)

    @pl.when(outer)
    def _():
        filter_quarter(mirror)
        pl.semaphore_wait(relay, 1)
        send_quarter(mirror)

    filter_quarter(mine)

    @pl.when(inner)
    def _():
        filter_quarter(beside)

        @pl.loop(0, chunks)
        def _(k):
            send_quarter_at(beside, k)
            send_near_at(k)

        send_front(split, chunks)

    @pl.when(outer)
    def _():
        @pl.loop(0, chunks)
        def _(k):
            @pl.when(k >= split)
            def _():
                send_front_at(k)
            send_near_at(k)

    @pl.when(outer)
    def _():
        filter_quarter(across)
        send_quarter(across)

    total = length * rows
    target_at = lax.broadcasted_iota(jnp.int32, (total, length), 0) // rows
    lane = lax.broadcasted_iota(jnp.int32, (total, length), 1)
    spread = jnp.sum(
        jnp.where(target_at == lane, widths_ref[...], 0.0), axis=1, keepdims=True
    )
    row_at = lax.broadcasted_iota(jnp.int32, (total, total), 0)
    col_at = lax.broadcasted_iota(jnp.int32, (total, total), 1)
    apart = row_at // rows - col_at // rows
    inside = (jnp.abs(apart) <= BAND) & (row_at % rows == col_at % rows)
    offset = apart.astype(jnp.float32)
    weights = jnp.where(
        inside, jnp.exp(-offset * offset / (2.0 * spread * spread)), 0.0
    )
    weights = weights / jnp.sum(weights, axis=1, keepdims=True)
    depth = total // LAYERS
    high = weights.astype(jnp.bfloat16)
    low = (weights - high.astype(jnp.float32)).astype(jnp.bfloat16)
    for layer in range(LAYERS):
        at = slice(layer * depth, (layer + 1) * depth)
        mixing[layer, :, 0:depth] = high[:, at]
        mixing[layer, :, depth : 2 * depth] = high[:, at]
        mixing[layer, :, 2 * depth : 3 * depth] = low[:, at]

    def share(k, layer):
        block = incoming.at[k, pl.ds(layer * quarter, quarter)]
        pltpu.make_async_copy(block, block, recv_sem.at[k, layer]).wait()
        if rows_block % 8 == 0:
            value = block[...].reshape(depth, chunk)
        else:
            value = jnp.concatenate([block[s] for s in range(quarter)], axis=0)
        value_high = value.astype(jnp.bfloat16)
        value_low = (value - value_high.astype(jnp.float32)).astype(jnp.bfloat16)
        return jnp.dot(
            mixing[layer],
            jnp.concatenate([value_high, value_low, value_high], axis=0),
            preferred_element_type=jnp.float32,
        )

    @pl.loop(0, chunks)
    def _(k):
        partial[...] = share(k, mine)
        partial[...] += share(k, beside)
        partial[...] += share(k, mirror)
        done = partial[...] + share(k, across)
        out_ref[:, :, pl.ds(pl.multiple_of(k * chunk, 128), chunk)] = done.reshape(
            length, rows, chunk
        )

    @pl.loop(0, chunks)
    def _(k):
        sent = outgoing.at[k, pl.ds(0, n - 1)]
        pltpu.make_async_copy(sent, sent, send_sem.at[k]).wait()


def write_kernel(mixed_ref, out_ref, sem):
    copy = pltpu.make_async_copy(mixed_ref, out_ref, sem)
    copy.start()
    copy.wait()


def in_hbm(array):
    return pltpu.with_memory_space_constraint(array, pltpu.HBM)


def local(n, frames, widths, kernel):
    per_device, height, columns = frames.shape
    length = widths.shape[0]
    rows = height // n
    chunk = 256 if columns % 256 == 0 else 128
    chunks = columns // chunk
    total = length * rows
    hbm = pl.BlockSpec(memory_space=pltpu.HBM)
    vmem = pl.BlockSpec(memory_space=pltpu.VMEM)
    shape = (length, rows, columns)
    rounds = 2 * (n // LAYERS).bit_length() + 1
    mixed = pl.pallas_call(
        functools.partial(exchange_kernel, n),
        out_shape=pltpu.VMEM(shape, jnp.float32),
        in_specs=[hbm] * 3,
        out_specs=vmem,
        scratch_shapes=[
            pltpu.VMEM((per_device, height + 16, columns), jnp.float32),
            pltpu.VMEM((per_device, height // LAYERS + 16, columns), jnp.float32),
            pltpu.VMEM((per_device, 24, columns), jnp.float32),
            pltpu.VMEM((chunks, n, per_device * rows, chunk), jnp.float32),
            pltpu.VMEM((chunks, n, per_device * rows, chunk), jnp.float32),
            pltpu.VMEM((LAYERS, total, 3 * total // LAYERS), jnp.bfloat16),
            pltpu.VMEM((total, chunk), jnp.float32),
            pltpu.VMEM((1, length), jnp.float32),
            pltpu.SMEM((3, 3), jnp.float32),
            pltpu.SemaphoreType.DMA((5,)),
            pltpu.SemaphoreType.DMA((chunks,)),
            pltpu.SemaphoreType.DMA((chunks, LAYERS)),
            pltpu.SemaphoreType.REGULAR((rounds,)),
        ],
        compiler_params=pltpu.CompilerParams(
            collective_id=0,
            has_side_effects=True,
            vmem_limit_bytes=50 * 1024 * 1024,
        ),
    )(in_hbm(frames), in_hbm(widths.reshape(1, length)), in_hbm(kernel))
    return pl.pallas_call(
        write_kernel,
        out_shape=pltpu.HBM(shape, jnp.float32),
        in_specs=[vmem],
        out_specs=hbm,
        scratch_shapes=[pltpu.SemaphoreType.DMA],
        compiler_params=pltpu.CompilerParams(vmem_limit_bytes=1024 * 1024),
    )(mixed)


def solution(mesh):
    return jax.shard_map(
        functools.partial(local, mesh.shape["blk"]),
        mesh=mesh,
        in_specs=(P("blk", None, None), P(), P()),
        out_specs=P(None, "blk", None),
        check_vma=False,
    )
```

time: 64.2 us -> 63.7 us (level)
  no operation moved by 1% of the time
where the time goes in v2:
time: 63.7 us; the launch traced here: 63.5 us
  Pallas kernels  63.5 us (100%)
    pallas_call x1, Pallas kernels, local(): pl.pallas_call(functools.partial(exchange_kernel, n), out_shape=pltpu.VME...  62 us
    pallas_call x1, Pallas kernels, local(): pl.pallas_call(write_kernel, out_shape=pltpu.HBM(shape, jnp.float32), in_...  1.5 us

profile of v2, /device:TPU:9, one launch (start us, length us, event | category | flops | bytes accessed | tf_op | source)
XLA Modules:
  0.0 63.5 jit_solution(3147942074554611113)
XLA Ops:
  0.0 62.0 %shard_map.37.mixed_ref = f32[128,4,1280]{2,1,0:T(4,128)S(1)} custom-call(f32[4,128,1280]{2,1,0:T(8,128)} %frames_ref.1, f32[1,128]{1,0:T(1,128)} %bitcast.1, f32[3,3]{1,0:T(4,128)} %kernel_hbm.1), custom_call_target="tpu_custom_call" | custom-call | tf_op jit(solution)/shard_map/pallas_call | solution.py:365
  62.0 1.5 %shard_map.38 = f32[128,4,1280]{2,1,0:T(4,128)} custom-call(f32[128,4,1280]{2,1,0:T(4,128)S(1)} %shard_map.37.mixed_ref), custom_call_target="tpu_custom_call" | custom-call | tf_op jit(solution)/shard_map/pallas_call | solution.py:391

commit v3 on v2

--- a/solution.py
+++ b/solution.py
@@ -18,6 +18,8 @@
     widths_hbm,
     kernel_hbm,
     out_ref,
+    last_ref,
+    rest_ref,
     held,
     window,
     opening,
@@ -65,6 +67,14 @@
     def mixed_seat(step):
         return lax.rem(seat + step, part)
 
+    def crossed_seat(step):
+        total = 0
+        for bit in range(bits):
+            width = 1 << bit
+            total = total + width * lax.rem(seat // width + step // width, 2)
+        return total
+
+    own = front * part + seat
     strip = height // LAYERS
     first = front * strip
 
@@ -75,15 +85,22 @@
             semaphore,
         )
 
+    taps_load = pltpu.make_async_copy(kernel_hbm, kernel_ref, in_sem.at[0])
+    top = pl.multiple_of(first + seat * 8 - 8, 8)
     early = [
-        pltpu.make_async_copy(kernel_hbm, kernel_ref, in_sem.at[0]),
-        load(first + seat * 8 - 8, 24, opening, 0, in_sem.at[1]),
+        pltpu.make_async_copy(
+            frames_ref.at[frame, pl.ds(top, 24), :],
+            opening.at[frame],
+            in_sem.at[4 + frame],
+        )
+        for frame in range(per_device)
     ]
-    front_load = load(first - 8, strip + 16, window, 0, in_sem.at[2])
+    front_load = load(first - 8, strip + 16, window, 0, in_sem.at[1])
     late = [
-        load(0, height, held, 8, in_sem.at[3]),
-        pltpu.make_async_copy(widths_hbm, widths_ref, in_sem.at[4]),
+        load(0, height, held, 8, in_sem.at[2]),
+        pltpu.make_async_copy(widths_hbm, widths_ref, in_sem.at[3]),
     ]
+    taps_load.start()
     for copy in early:
         copy.start()
 
@@ -108,32 +125,33 @@
     held[:, pl.ds(height + 8, 8), :] = edge
     column = lax.broadcasted_iota(jnp.int32, (8, columns), 1)
 
+    def filter_frame(at, source, frame, start):
+        tall = source[frame, pl.ds(start, 24), :]
+        taps = [tall[7:15], tall[8:16], tall[9:17]]
+        mixed = [
+            kernel_ref[0, col] * taps[0]
+            + kernel_ref[1, col] * taps[1]
+            + kernel_ref[2, col] * taps[2]
+            for col in range(3)
+        ]
+        left = jnp.where(column == 0, 0.0, pltpu.roll(mixed[0], 1, 1))
+        right = jnp.where(
+            column == columns - 1, 0.0, pltpu.roll(mixed[2], columns - 1, 1)
+        )
+        value = left + mixed[1] + right
+        for member in range(group):
+            for k in range(chunks):
+                outgoing[
+                    k, at * group + member, pl.ds(frame * rows, rows), :
+                ] = value[
+                    member * rows : (member + 1) * rows,
+                    k * chunk : (k + 1) * chunk,
+                ]
+
     def filter_group(at, source, base):
+        start = pl.multiple_of((at - base) * 8, 8)
         for frame in range(per_device):
-            start = (at - base) * 8
-            if not isinstance(start, int):
-                start = pl.multiple_of(start, 8)
-            tall = source[frame, pl.ds(start, 24), :]
-            taps = [tall[7:15], tall[8:16], tall[9:17]]
-            mixed = [
-                kernel_ref[0, col] * taps[0]
-                + kernel_ref[1, col] * taps[1]
-                + kernel_ref[2, col] * taps[2]
-                for col in range(3)
-            ]
-            left = jnp.where(column == 0, 0.0, pltpu.roll(mixed[0], 1, 1))
-            right = jnp.where(
-                column == columns - 1, 0.0, pltpu.roll(mixed[2], columns - 1, 1)
-            )
-            value = left + mixed[1] + right
-            for member in range(group):
-                for k in range(chunks):
-                    outgoing[
-                        k, at * group + member, pl.ds(frame * rows, rows), :
-                    ] = value[
-                        member * rows : (member + 1) * rows,
-                        k * chunk : (k + 1) * chunk,
-                    ]
+            filter_frame(at, source, frame, start)
 
     def send(k, target):
         pltpu.make_async_remote_copy(
@@ -146,7 +164,7 @@
         ).start()
 
     def send_group(at):
-        @pl.loop(0, chunks)
+        @pl.loop(0, 4)
         def _(k):
             for member in range(group):
                 send(k, at * group + member)
@@ -169,6 +187,11 @@
             at = front * part + mixed_seat(step)
             for member in range(group):
                 send(k, at * group + member)
+
+        @pl.when(outer | (k >= 4))
+        def _():
+            for member in range(group):
+                send(k, own * group + member)
 
     def send_front(begin, end):
         @pl.loop(begin, end)
@@ -198,15 +221,15 @@
         def _(step):
             filter_group(which * part + mixed_seat(step), held, 0)
 
-    for copy in early:
-        copy.wait()
+    taps_load.wait()
+    for frame in range(per_device):
+        early[frame].wait()
+        filter_frame(own, opening, frame, 0)
     front_load.start()
     for copy in late:
         copy.start()
-    own = front * part + seat
-    filter_group(own, opening, own)
     pl.semaphore_wait(barrier, group + core_bits + bits)
-    send_group(own)
+    pl.when(inner)(lambda: send_group(own))
 
     @pl.when(outer)
     def _():
@@ -225,12 +248,19 @@
 
         @pl.loop(1 << bit, 2 << bit)
         def _(step):
-            filter_group(front * part + mixed_seat(step), window, front * part)
+            filter_group(front * part + crossed_seat(step), window, front * part)
 
         pl.semaphore_wait(at, 1)
 
+        @pl.when(inner)
+        def _():
+            @pl.loop(1 << bit, 2 << bit)
+            def _(step):
+                for member in range(group):
+                    send(0, (front * part + crossed_seat(step)) * group + member)
+
     split = jnp.where(inner, min(2, chunks), 0)
-    send_front(0, split)
+    send_front(1, split)
     for copy in late:
         copy.wait()
 
@@ -253,12 +283,6 @@
         signal(relay, partner)
         send_quarter(across)
 
-    @pl.when(outer)
-    def _():
-        filter_quarter(mirror)
-        pl.semaphore_wait(relay, 1)
-        send_quarter(mirror)
-
     filter_quarter(mine)
 
     @pl.when(inner)
@@ -274,11 +298,13 @@
 
     @pl.when(outer)
     def _():
+        filter_quarter(mirror)
+        pl.semaphore_wait(relay, 1)
+
         @pl.loop(0, chunks)
         def _(k):
-            @pl.when(k >= split)
-            def _():
-                send_front_at(k)
+            send_quarter_at(mirror, k)
+            send_front_at(k)
             send_near_at(k)
 
     @pl.when(outer)
@@ -310,30 +336,46 @@
         mixing[layer, :, depth : 2 * depth] = high[:, at]
         mixing[layer, :, 2 * depth : 3 * depth] = low[:, at]
 
-    def share(k, layer):
+    last_ref[...] = mixing[mirror]
+
+    def arrive(k, layer):
         block = incoming.at[k, pl.ds(layer * quarter, quarter)]
         pltpu.make_async_copy(block, block, recv_sem.at[k, layer]).wait()
+        return block
+
+    def share(k, layer):
+        block = arrive(k, layer)
         if rows_block % 8 == 0:
             value = block[...].reshape(depth, chunk)
         else:
             value = jnp.concatenate([block[s] for s in range(quarter)], axis=0)
-        value_high = value.astype(jnp.bfloat16)
-        value_low = (value - value_high.astype(jnp.float32)).astype(jnp.bfloat16)
-        return jnp.dot(
-            mixing[layer],
-            jnp.concatenate([value_high, value_low, value_high], axis=0),
-            preferred_element_type=jnp.float32,
+        return product(mixing[layer], value)
+
+    def put(k, value):
+        out_ref[:, :, pl.ds(pl.multiple_of(k * chunk, 128), chunk)] = value.reshape(
+            length, rows, chunk
         )
 
     @pl.loop(0, chunks)
     def _(k):
         partial[...] = share(k, mine)
         partial[...] += share(k, beside)
-        partial[...] += share(k, mirror)
-        done = partial[...] + share(k, across)
-        out_ref[:, :, pl.ds(pl.multiple_of(k * chunk, 128), chunk)] = done.reshape(
-            length, rows, chunk
-        )
+
+        @pl.when(k < chunks - 1)
+        def _():
+            partial[...] += share(k, across)
+            put(k, partial[...] + share(k, mirror))
+
+        @pl.when(k == chunks - 1)
+        def _():
+            put(k, partial[...] + share(k, across))
+
+    block = arrive(chunks - 1, mirror)
+    if rows_block % 8 == 0:
+        value = block[...].reshape(depth, chunk)
+    else:
+        value = jnp.concatenate([block[s] for s in range(quarter)], axis=0)
+    rest_ref[...] = value
 
     @pl.loop(0, chunks)
     def _(k):
@@ -341,10 +383,33 @@
         pltpu.make_async_copy(sent, sent, send_sem.at[k]).wait()
 
 
-def write_kernel(mixed_ref, out_ref, sem):
-    copy = pltpu.make_async_copy(mixed_ref, out_ref, sem)
-    copy.start()
-    copy.wait()
+def product(weights, value):
+    high = value.astype(jnp.bfloat16)
+    low = (value - high.astype(jnp.float32)).astype(jnp.bfloat16)
+    return jnp.dot(
+        weights,
+        jnp.concatenate([high, low, high], axis=0),
+        preferred_element_type=jnp.float32,
+    )
+
+
+def write_kernel(mixed_ref, last_ref, rest_ref, out_ref, end, sem):
+    length, rows, columns = mixed_ref.shape
+    chunk = rest_ref.shape[1]
+    begin = columns - chunk
+    ready = pltpu.make_async_copy(
+        mixed_ref.at[:, :, pl.ds(0, begin)],
+        out_ref.at[:, :, pl.ds(0, begin)],
+        sem.at[0],
+    )
+    ready.start()
+    end[...] = mixed_ref[:, :, begin:] + product(
+        last_ref[...], rest_ref[...]
+    ).reshape(length, rows, chunk)
+    final = pltpu.make_async_copy(end, out_ref.at[:, :, pl.ds(begin, chunk)], sem.at[1])
+    final.start()
+    ready.wait()
+    final.wait()
 
 
 def in_hbm(array):
@@ -358,15 +423,20 @@
     chunk = 256 if columns % 256 == 0 else 128
     chunks = columns // chunk
     total = length * rows
+    depth = total // LAYERS
     hbm = pl.BlockSpec(memory_space=pltpu.HBM)
     vmem = pl.BlockSpec(memory_space=pltpu.VMEM)
     shape = (length, rows, columns)
     rounds = 2 * (n // LAYERS).bit_length() + 1
     mixed = pl.pallas_call(
         functools.partial(exchange_kernel, n),
-        out_shape=pltpu.VMEM(shape, jnp.float32),
+        out_shape=(
+            pltpu.VMEM(shape, jnp.float32),
+            pltpu.VMEM((total, 3 * depth), jnp.bfloat16),
+            pltpu.VMEM((depth, chunk), jnp.float32),
+        ),
         in_specs=[hbm] * 3,
-        out_specs=vmem,
+        out_specs=(vmem, vmem, vmem),
         scratch_shapes=[
             pltpu.VMEM((per_device, height + 16, columns), jnp.float32),
             pltpu.VMEM((per_device, height // LAYERS + 16, columns), jnp.float32),
@@ -377,7 +447,7 @@
             pltpu.VMEM((total, chunk), jnp.float32),
             pltpu.VMEM((1, length), jnp.float32),
             pltpu.SMEM((3, 3), jnp.float32),
-            pltpu.SemaphoreType.DMA((5,)),
+            pltpu.SemaphoreType.DMA((4 + per_device,)),
             pltpu.SemaphoreType.DMA((chunks,)),
             pltpu.SemaphoreType.DMA((chunks, LAYERS)),
             pltpu.SemaphoreType.REGULAR((rounds,)),
@@ -391,11 +461,14 @@
     return pl.pallas_call(
         write_kernel,
         out_shape=pltpu.HBM(shape, jnp.float32),
-        in_specs=[vmem],
+        in_specs=[vmem] * 3,
         out_specs=hbm,
-        scratch_shapes=[pltpu.SemaphoreType.DMA],
-        compiler_params=pltpu.CompilerParams(vmem_limit_bytes=1024 * 1024),
-    )(mixed)
+        scratch_shapes=[
+            pltpu.VMEM((length, rows, chunk), jnp.float32),
+            pltpu.SemaphoreType.DMA((2,)),
+        ],
+        compiler_params=pltpu.CompilerParams(vmem_limit_bytes=4 * 1024 * 1024),
+    )(*mixed)
 
 
 def solution(mesh):

time: 63.7 us -> 62.6 us (0.983)
  Pallas kernels: 63.5 us -> 62.4 us
    pallas_call x1, Pallas kernels: 62 us -> 60.9 us  [local(): pl.pallas_call(functools.partial(exchange_kernel, n), out_shape=(pltpu.VM...]
where the time goes in v3:
time: 62.6 us; the launch traced here: 62.4 us
  Pallas kernels  62.4 us (100%)
    pallas_call x1, Pallas kernels, local(): pl.pallas_call(functools.partial(exchange_kernel, n), out_shape=(pltpu.VM...  60.9 us
    pallas_call x1, Pallas kernels, local(): pl.pallas_call(write_kernel, out_shape=pltpu.HBM(shape, jnp.float32), in_...  1.51 us

profile of v3, /device:TPU:9, one launch (start us, length us, event | category | flops | bytes accessed | tf_op | source)
XLA Modules:
  0.0 62.4 jit_solution(9969683272210841409)
XLA Ops:
  0.0 60.9 %shard_map.37 = (f32[128,4,1280]{2,1,0:T(4,128)S(1)}, bf16[512,384]{1,0:T(8,128)(2,1)S(1)}, f32[128,256]{1,0:T(8,128)S(1)}) custom-call(f32[4,128,1280]{2,1,0:T(8,128)} %frames_ref.1, f32[1,128]{1,0:T(1,128)} %bitcast.1, f32[3,3]{1,0:T(4,128)} %kernel_hbm.1), custom_call_target="tpu_custom_call" | custom-call | tf_op jit(solution)/shard_map/pallas_call | solution.py:431
  60.9 1.5 %shard_map.38 = f32[128,4,1280]{2,1,0:T(4,128)} custom-call(f32[128,4,1280]{2,1,0:T(4,128)S(1)} %get-tuple-element.8.mixed_ref, bf16[512,384]{1,0:T(8,128)(2,1)S(1)} %get-tuple-element.9.last_ref, f32[128,256]{1,0:T(8,128)S(1)} %get-tuple-element.10.rest_ref), custom_call_target="tpu_custom_call" | custom-call | tf_op jit(solution)/shard_map/pallas_call | solution.py:461

commit v4 on v3

--- a/solution.py
+++ b/solution.py
@@ -38,6 +38,7 @@
     chunks, _, rows_block, chunk = outgoing.shape
     rows = rows_block // per_device
     group = 8 // rows
+    held_back = max(chunks - 1, 1)
     length = widths_ref.shape[1]
     me = lax.axis_index("blk")
     quarter = n // LAYERS
@@ -87,13 +88,15 @@
 
     taps_load = pltpu.make_async_copy(kernel_hbm, kernel_ref, in_sem.at[0])
     top = pl.multiple_of(first + seat * 8 - 8, 8)
+    margin = min(chunk + 128, columns)
+    edges = [(0, margin)] + ([(margin, columns)] if margin < columns else [])
     early = [
         pltpu.make_async_copy(
-            frames_ref.at[frame, pl.ds(top, 24), :],
-            opening.at[frame],
-            in_sem.at[4 + frame],
+            frames_ref.at[:, pl.ds(top, 24), pl.ds(begin, end - begin)],
+            opening.at[:, :, pl.ds(begin, end - begin)],
+            in_sem.at[4 + at],
         )
-        for frame in range(per_device)
+        for at, (begin, end) in enumerate(edges)
     ]
     front_load = load(first - 8, strip + 16, window, 0, in_sem.at[1])
     late = [
@@ -103,6 +106,7 @@
     taps_load.start()
     for copy in early:
         copy.start()
+    front_load.start()
 
     def signal(semaphore, target):
         pl.semaphore_signal(
@@ -123,10 +127,12 @@
     edge = jnp.zeros((per_device, 8, columns), jnp.float32)
     held[:, pl.ds(0, 8), :] = edge
     held[:, pl.ds(height + 8, 8), :] = edge
-    column = lax.broadcasted_iota(jnp.int32, (8, columns), 1)
-
-    def filter_frame(at, source, frame, start):
-        tall = source[frame, pl.ds(start, 24), :]
+
+    def filter_frame(at, source, frame, start, begin=0, end=None):
+        end = columns if end is None else end
+        low, high = max(begin - 128, 0), min(end + 128, columns)
+        wide = high - low
+        tall = source[frame, pl.ds(start, 24), low:high]
         taps = [tall[7:15], tall[8:16], tall[9:17]]
         mixed = [
             kernel_ref[0, col] * taps[0]
@@ -134,18 +140,21 @@
             + kernel_ref[2, col] * taps[2]
             for col in range(3)
         ]
-        left = jnp.where(column == 0, 0.0, pltpu.roll(mixed[0], 1, 1))
-        right = jnp.where(
-            column == columns - 1, 0.0, pltpu.roll(mixed[2], columns - 1, 1)
-        )
+        left = pltpu.roll(mixed[0], 1, 1)
+        right = pltpu.roll(mixed[2], wide - 1, 1)
+        lane = lax.broadcasted_iota(jnp.int32, (8, wide), 1) + low
+        if low == 0:
+            left = jnp.where(lane == 0, 0.0, left)
+        if high == columns:
+            right = jnp.where(lane == columns - 1, 0.0, right)
         value = left + mixed[1] + right
         for member in range(group):
-            for k in range(chunks):
+            for k in range(begin // chunk, end // chunk):
                 outgoing[
                     k, at * group + member, pl.ds(frame * rows, rows), :
                 ] = value[
                     member * rows : (member + 1) * rows,
-                    k * chunk : (k + 1) * chunk,
+                    k * chunk - low : (k + 1) * chunk - low,
                 ]
 
     def filter_group(at, source, base):
@@ -164,7 +173,7 @@
         ).start()
 
     def send_group(at):
-        @pl.loop(0, 4)
+        @pl.loop(1, held_back)
         def _(k):
             for member in range(group):
                 send(k, at * group + member)
@@ -172,7 +181,7 @@
     def send_quarter_at(which, k):
         @pl.loop(0, part)
         def _(step):
-            at = which * part + mixed_seat(step)
+            at = which * part + lax.rem(seat + part + step * (1 - 2 * lax.rem(me, 2)), part)
             for member in range(group):
                 send(k, at * group + member)
 
@@ -188,7 +197,7 @@
             for member in range(group):
                 send(k, at * group + member)
 
-        @pl.when(outer | (k >= 4))
+        @pl.when(outer | (k >= held_back))
         def _():
             for member in range(group):
                 send(k, own * group + member)
@@ -222,14 +231,23 @@
             filter_group(which * part + mixed_seat(step), held, 0)
 
     taps_load.wait()
+    early[0].wait()
     for frame in range(per_device):
-        early[frame].wait()
-        filter_frame(own, opening, frame, 0)
-    front_load.start()
+        filter_frame(own, opening, frame, 0, 0, chunk)
+    pl.semaphore_wait(barrier, group + steps)
+
+    @pl.when(inner)
+    def _():
+        for member in range(group):
+            send(0, own * group + member)
+
+    if chunks > 1:
+        early[-1].wait()
+        for frame in range(per_device):
+            filter_frame(own, opening, frame, 0, chunk, columns)
+        pl.when(inner)(lambda: send_group(own))
     for copy in late:
         copy.start()
-    pl.semaphore_wait(barrier, group + core_bits + bits)
-    pl.when(inner)(lambda: send_group(own))
 
     @pl.when(outer)
     def _():
@@ -241,10 +259,11 @@
     for bit in range(core_bits):
         pass_on(bit, round_sem.at[bit])
         pl.semaphore_wait(round_sem.at[bit], 1)
-    front_load.wait()
     for bit in range(bits):
         at = round_sem.at[core_bits + bit]
         pass_on(core_bits + bit, at)
+        if bit == 0:
+            front_load.wait()
 
         @pl.loop(1 << bit, 2 << bit)
         def _(step):
@@ -281,9 +300,10 @@
 
         pl.semaphore_wait(meet, 1)
         signal(relay, partner)
+        filter_quarter(mine)
         send_quarter(across)
 
-    filter_quarter(mine)
+    pl.when(outer)(lambda: filter_quarter(mine))
 
     @pl.when(inner)
     def _():
@@ -447,7 +467,7 @@
             pltpu.VMEM((total, chunk), jnp.float32),
             pltpu.VMEM((1, length), jnp.float32),
             pltpu.SMEM((3, 3), jnp.float32),
-            pltpu.SemaphoreType.DMA((4 + per_device,)),
+            pltpu.SemaphoreType.DMA((6,)),
             pltpu.SemaphoreType.DMA((chunks,)),
             pltpu.SemaphoreType.DMA((chunks, LAYERS)),
             pltpu.SemaphoreType.REGULAR((rounds,)),

time: 62.6 us -> 62.4 us (level)
  no operation moved by 1% of the time
where the time goes in v4:
time: 62.4 us; the launch traced here: 62.3 us
  Pallas kernels  62.3 us (100%)
    pallas_call x1, Pallas kernels, local(): pl.pallas_call(functools.partial(exchange_kernel, n), out_shape=(pltpu.VM...  60.8 us
    pallas_call x1, Pallas kernels, local(): pl.pallas_call(write_kernel, out_shape=pltpu.HBM(shape, jnp.float32), in_...  1.51 us

profile of v4, /device:TPU:9, one launch (start us, length us, event | category | flops | bytes accessed | tf_op | source)
XLA Modules:
  0.0 62.3 jit_solution(18099332903656107810)
XLA Ops:
  0.0 60.8 %shard_map.37 = (f32[128,4,1280]{2,1,0:T(4,128)S(1)}, bf16[512,384]{1,0:T(8,128)(2,1)S(1)}, f32[128,256]{1,0:T(8,128)S(1)}) custom-call(f32[4,128,1280]{2,1,0:T(8,128)} %frames_ref.1, f32[1,128]{1,0:T(1,128)} %bitcast.1, f32[3,3]{1,0:T(4,128)} %kernel_hbm.1), custom_call_target="tpu_custom_call" | custom-call | tf_op jit(solution)/shard_map/pallas_call | solution.py:451
  60.8 1.5 %shard_map.38 = f32[128,4,1280]{2,1,0:T(4,128)} custom-call(f32[128,4,1280]{2,1,0:T(4,128)S(1)} %get-tuple-element.8.mixed_ref, bf16[512,384]{1,0:T(8,128)(2,1)S(1)} %get-tuple-element.9.last_ref, f32[128,256]{1,0:T(8,128)S(1)} %get-tuple-element.10.rest_ref), custom_call_target="tpu_custom_call" | custom-call | tf_op jit(solution)/shard_map/pallas_call | solution.py:481

commit v5 on v4

--- a/solution.py
+++ b/solution.py
@@ -193,13 +193,16 @@
     def send_front_at(k):
         @pl.loop(1, part)
         def _(step):
-            at = front * part + mixed_seat(step)
+            seat_at = jnp.where(
+                k >= held_back, crossed_seat(part - step), mixed_seat(step)
+            )
+            at = front * part + seat_at
             for member in range(group):
                 send(k, at * group + member)
 
         @pl.when(outer | (k >= held_back))
         def _():
-            for member in range(group):
+            for member in reversed(range(group)):
                 send(k, own * group + member)
 
     def send_front(begin, end):

time: 62.4 us -> 62.4 us (level)
  no operation moved by 1% of the time
where the time goes in v5:
time: 62.4 us; the launch traced here: 62.3 us
  Pallas kernels  62.3 us (100%)
    pallas_call x1, Pallas kernels, local(): pl.pallas_call(functools.partial(exchange_kernel, n), out_shape=(pltpu.VM...  60.8 us
    pallas_call x1, Pallas kernels, local(): pl.pallas_call(write_kernel, out_shape=pltpu.HBM(shape, jnp.float32), in_...  1.51 us

profile of v5, /device:TPU:9, one launch (start us, length us, event | category | flops | bytes accessed | tf_op | source)
XLA Modules:
  0.0 62.3 jit_solution(4241702030995624111)
XLA Ops:
  0.0 60.8 %shard_map.37 = (f32[128,4,1280]{2,1,0:T(4,128)S(1)}, bf16[512,384]{1,0:T(8,128)(2,1)S(1)}, f32[128,256]{1,0:T(8,128)S(1)}) custom-call(f32[4,128,1280]{2,1,0:T(8,128)} %frames_ref.1, f32[1,128]{1,0:T(1,128)} %bitcast.1, f32[3,3]{1,0:T(4,128)} %kernel_hbm.1), custom_call_target="tpu_custom_call" | custom-call | tf_op jit(solution)/shard_map/pallas_call | solution.py:454
  60.8 1.5 %shard_map.38 = f32[128,4,1280]{2,1,0:T(4,128)} custom-call(f32[128,4,1280]{2,1,0:T(4,128)S(1)} %get-tuple-element.8.mixed_ref, bf16[512,384]{1,0:T(8,128)(2,1)S(1)} %get-tuple-element.9.last_ref, f32[128,256]{1,0:T(8,128)S(1)} %get-tuple-element.10.rest_ref), custom_call_target="tpu_custom_call" | custom-call | tf_op jit(solution)/shard_map/pallas_call | solution.py:484

commit v6 on v5

--- a/solution.py
+++ b/solution.py
@@ -393,17 +393,17 @@
         def _():
             put(k, partial[...] + share(k, across))
 
+    @pl.loop(0, chunks)
+    def _(k):
+        sent = outgoing.at[k, pl.ds(0, n - 1)]
+        pltpu.make_async_copy(sent, sent, send_sem.at[k]).wait()
+
     block = arrive(chunks - 1, mirror)
     if rows_block % 8 == 0:
         value = block[...].reshape(depth, chunk)
     else:
         value = jnp.concatenate([block[s] for s in range(quarter)], axis=0)
     rest_ref[...] = value
-
-    @pl.loop(0, chunks)
-    def _(k):
-        sent = outgoing.at[k, pl.ds(0, n - 1)]
-        pltpu.make_async_copy(sent, sent, send_sem.at[k]).wait()
 
 
 def product(weights, value):

time: 62.4 us -> 62.4 us (level)
  no operation moved by 1% of the time
where the time goes in v6:
time: 62.4 us; the launch traced here: 62.2 us
  Pallas kernels  62.2 us (100%)
    pallas_call x1, Pallas kernels, local(): pl.pallas_call(functools.partial(exchange_kernel, n), out_shape=(pltpu.VM...  60.7 us
    pallas_call x1, Pallas kernels, local(): pl.pallas_call(write_kernel, out_shape=pltpu.HBM(shape, jnp.float32), in_...  1.51 us

profile of v6, /device:TPU:9, one launch (start us, length us, event | category | flops | bytes accessed | tf_op | source)
XLA Modules:
  0.0 62.2 jit_solution(14448778136495966996)
XLA Ops:
  0.0 60.7 %shard_map.37 = (f32[128,4,1280]{2,1,0:T(4,128)S(1)}, bf16[512,384]{1,0:T(8,128)(2,1)S(1)}, f32[128,256]{1,0:T(8,128)S(1)}) custom-call(f32[4,128,1280]{2,1,0:T(8,128)} %frames_ref.1, f32[1,128]{1,0:T(1,128)} %bitcast.1, f32[3,3]{1,0:T(4,128)} %kernel_hbm.1), custom_call_target="tpu_custom_call" | custom-call | tf_op jit(solution)/shard_map/pallas_call | solution.py:454
  60.7 1.5 %shard_map.38 = f32[128,4,1280]{2,1,0:T(4,128)} custom-call(f32[128,4,1280]{2,1,0:T(4,128)S(1)} %get-tuple-element.8.mixed_ref, bf16[512,384]{1,0:T(8,128)(2,1)S(1)} %get-tuple-element.9.last_ref, f32[128,256]{1,0:T(8,128)S(1)} %get-tuple-element.10.rest_ref), custom_call_target="tpu_custom_call" | custom-call | tf_op jit(solution)/shard_map/pallas_call | solution.py:484
